TPU v7x, 32 devices: a whole 2x2x4 slice. The times are simulated.
32 devices in a mesh: ctx: 16 (over z, y, x), tp: 2 (over core).
Axes of the slice: x: 2, y: 2, z: 4, core: 2. Of those that a mesh axis runs over, the one named last changes fastest.
Arguments:
- byte_states: bfloat16 [4096, 1024], P('ctx'), may hold values from -12 to 12, as said below
- patch_of_byte: int32 [4096], P('ctx'), may hold values from 0 to 125, as said below
- patch_first: int32 [16], replicated, may hold values from 0 to 991, as said below
- moved: int32 [2, 16], replicated, may hold values from 0 to 32, as said below
- w_qkv: bfloat16 [3, 1024, 2048], P(None, None, 'tp'), may hold values from -0.25 to 0.25, as said below
- d_attn: bfloat16 [1024, 2048], P('ctx', 'tp'), may hold values from -6 to 6
Outputs:
- attn_out: bfloat16 [1024, 2048], P('ctx', 'tp')
- byte_grad: bfloat16 [4096, 1024], P('ctx', 'tp')
Inputs may be any that keep to these rules, and one draw needn't show every extreme that they name: `patch_of_byte`: within each byte shard the numbers start at 0 and rise by 0 or 1 from byte to byte; a shard holds at most 126 patches, reached on some shard. `patch_first`: the sum of the patch counts of all earlier byte shards; shard 0 starts at 0. moved[0, 0] = 0 and moved[1, 15] = 0; every other entry is 1 to 32; every patch shard thereby receives exactly 64 patches, and the patch counts agree with patch_first and patch_of_byte. `w_qkv`: independent entries of order 1024 ** -0.5. `byte_states`: entries of order one.
All inputs are finite; a program needn't handle non-finite values.
Results may differ from a plain program's by a relative error of at most 0.011.
Values may be sent and summed in bfloat16 or wider, within the bound.
A program may use at most 64 MiB of HBM per device.

v0:
```python
import jax
import jax.numpy as jnp
from jax import lax
from jax.sharding import PartitionSpec as P

HD = 128


def extended_2(x, sides, width):
    for axis, dim in sides:
        peers, length = (lax.axis_size(axis), x.shape[dim])
        up = [(i, (i + 1) % peers) for i in range(peers - 1)]
        down = [(j, i) for i, j in up]
        last = lax.slice_in_dim(x, length - width, length, axis=dim)
        first = lax.slice_in_dim(x, 0, width, axis=dim)
        before = lax.ppermute(last, axis, up)
        after = lax.ppermute(first, axis, down)
        x = jnp.concatenate([before, x, after], axis=dim)
    return x


def pick_own(values, index):
    return lax.dynamic_index_in_dim(values, index, 0, keepdims=False)


def shards(byte_states, patch_of_byte, patch_first, moved, w_qkv, d_attn):
    ctx_index = lax.axis_index("ctx")
    n_ctx = lax.axis_size("ctx")
    rows = d_attn.shape[0]
    feats = d_attn.shape[1]
    heads = feats // HD
    capacity = 2 * rows
    total = rows * n_ctx
    scale = HD ** (-0.5)
    ends = jnp.concatenate([patch_first[1:], jnp.full((1,), total, jnp.int32)])
    counts = ends - patch_first
    lower_moves = moved[0]
    upper_moves = moved[1]
    zero_one = jnp.zeros((1,), jnp.int32)
    below_high = jnp.concatenate([zero_one, upper_moves[:-1]])
    above_low = jnp.concatenate([lower_moves[1:], zero_one])
    prev_first = jnp.concatenate([zero_one, patch_first[:-1]])
    prev_count = jnp.concatenate([zero_one, counts[:-1]])
    ranks = jnp.arange(rows, dtype=jnp.int32)[None, :]
    from_low = ranks < below_high[:, None]
    from_high = ranks >= (rows - above_low)[:, None]
    lower_local = prev_count[:, None] - below_high[:, None] + ranks
    own_local = lower_moves[:, None] + ranks - below_high[:, None]
    upper_local = ranks - (rows - above_low)[:, None]
    ids_all = jnp.where(
        from_low,
        prev_first[:, None] + lower_local,
        jnp.where(from_high, ends[:, None] + upper_local, patch_first[:, None] + own_local),
    )
    source_all = jnp.where(
        from_low,
        lower_local,
        jnp.where(from_high, 2 * capacity + upper_local, capacity + own_local),
    )
    wanted = pick_own(ids_all, ctx_index)
    source_rows = pick_own(source_all, ctx_index)
    key_place = ids_all.reshape(-1)
    slots = jnp.arange(capacity, dtype=jnp.int32)
    member = patch_of_byte[None, :] == slots[:, None]
    lengths = jnp.sum(member.astype(jnp.float32), axis=1)
    onehot = member.astype(jnp.bfloat16)
    part = byte_states.shape[1] // lax.axis_size("tp")
    source = lax.dynamic_slice_in_dim(byte_states, lax.axis_index("tp") * part, part, 1)
    pooled_local = (
        jnp.dot(onehot, source, preferred_element_type=jnp.float32)
        / jnp.maximum(lengths, 1.0)[:, None]
    ).astype(jnp.bfloat16)
    extended = extended_2(pooled_local, (("ctx", 0),), capacity)
    picker = (source_rows[:, None] == jnp.arange(3 * capacity, dtype=jnp.int32)[None, :]).astype(
        jnp.bfloat16
    )
    pooled = jnp.dot(picker, extended, preferred_element_type=jnp.float32).astype(jnp.bfloat16)
    pooled = lax.all_gather(pooled, "tp", axis=1, tiled=True)
    query = jnp.dot(pooled, w_qkv[0], preferred_element_type=jnp.float32).astype(jnp.bfloat16)
    keyed = jnp.dot(pooled, w_qkv[1], preferred_element_type=jnp.float32).astype(jnp.bfloat16)
    valued = jnp.dot(pooled, w_qkv[2], preferred_element_type=jnp.float32).astype(jnp.bfloat16)
    keys_all, values_all = (
        lax.all_gather(keyed, "ctx", axis=0, tiled=True),
        lax.all_gather(valued, "ctx", axis=0, tiled=True),
    )
    query3 = query.reshape(rows, heads, HD)
    keys3 = keys_all.reshape(total, heads, HD)
    values3 = values_all.reshape(total, heads, HD)
    causal = (wanted[:, None] >= key_place[None, :])[None, :, :]
    score = jnp.einsum("qhd,khd->hqk", query3, keys3, preferred_element_type=jnp.float32) * scale
    masked = jnp.where(causal, score, -jnp.inf)
    top = jnp.max(masked, axis=2, keepdims=True)
    lse = top + jnp.log(jnp.sum(jnp.exp(masked - top), axis=2, keepdims=True))
    prob = jnp.exp(jnp.where(causal, score - lse, -jnp.inf))
    probs = prob.astype(jnp.bfloat16)
    output3 = jnp.einsum("hqk,khd->qhd", probs, values3, preferred_element_type=jnp.float32).astype(
        jnp.bfloat16
    )
    attn_out = output3.reshape(rows, feats)
    grad3 = d_attn.reshape(rows, heads, HD)
    delta = jnp.sum(grad3.astype(jnp.float32) * output3.astype(jnp.float32), axis=2)
    dprob = jnp.einsum("qhd,khd->hqk", grad3, values3, preferred_element_type=jnp.float32)
    dscore = (prob * (dprob - jnp.transpose(delta)[:, :, None])).astype(jnp.bfloat16)
    d_query = (
        jnp.einsum("hqk,khd->qhd", dscore, keys3, preferred_element_type=jnp.float32) * scale
    ).astype(jnp.bfloat16)
    lse_rows = jnp.transpose(lse[:, :, 0])
    lse_all, delta_all = (
        lax.all_gather(lse_rows, "ctx", axis=0, tiled=True),
        lax.all_gather(delta, "ctx", axis=0, tiled=True),
    )
    own_keys = keyed.reshape(rows, heads, HD)
    own_values = valued.reshape(rows, heads, HD)
    q_piece = lax.all_gather(query, "ctx", axis=0, tiled=True)
    g_piece = lax.all_gather(d_attn, "ctx", axis=0, tiled=True)
    count = q_piece.shape[0]
    q_three = q_piece.reshape(count, heads, HD)
    g_three = g_piece.reshape(count, heads, HD)
    lse_piece = jnp.transpose(lse_all)
    delta_piece = jnp.transpose(delta_all)
    allowed = (key_place[:, None] >= wanted[None, :])[None, :, :]
    part_score = (
        jnp.einsum("qhd,khd->hqk", q_three, own_keys, preferred_element_type=jnp.float32) * scale
    )
    part_prob = jnp.exp(jnp.where(allowed, part_score - lse_piece[:, :, None], -jnp.inf))
    part_probs = part_prob.astype(jnp.bfloat16)
    d_value_sum = jnp.einsum(
        "hqk,qhd->khd", part_probs, g_three, preferred_element_type=jnp.float32
    )
    part_dprob = jnp.einsum("qhd,khd->hqk", g_three, own_values, preferred_element_type=jnp.float32)
    part_dscore = (part_prob * (part_dprob - delta_piece[:, :, None])).astype(jnp.bfloat16)
    d_key_sum = (
        jnp.einsum("hqk,qhd->khd", part_dscore, q_three, preferred_element_type=jnp.float32) * scale
    )
    d_key_sum, d_value_sum = (d_key_sum, d_value_sum)
    d_key = d_key_sum.astype(jnp.bfloat16).reshape(rows, feats)
    d_value = d_value_sum.astype(jnp.bfloat16).reshape(rows, feats)
    d_query = d_query.reshape(rows, feats)
    contract = (((1,), (1,)), ((), ()))
    partial_value = lax.dot_general(d_query, w_qkv[0], contract, preferred_element_type=jnp.float32)
    partial_value = partial_value + lax.dot_general(
        d_key, w_qkv[1], contract, preferred_element_type=jnp.float32
    )
    partial_value = partial_value + lax.dot_general(
        d_value, w_qkv[2], contract, preferred_element_type=jnp.float32
    )
    d_pooled = lax.psum_scatter(partial_value, "tp", scatter_dimension=1, tiled=True).astype(
        jnp.bfloat16
    )
    returned = extended_2(d_pooled, (("ctx", 0),), rows)
    my_count = pick_own(counts, ctx_index)
    my_low = pick_own(lower_moves, ctx_index)
    my_high = pick_own(upper_moves, ctx_index)
    my_below = pick_own(below_high, ctx_index)
    target = jnp.where(
        patch_of_byte < my_low,
        rows - my_low + patch_of_byte,
        jnp.where(
            patch_of_byte >= my_count - my_high,
            2 * rows + patch_of_byte - (my_count - my_high),
            rows + my_below + patch_of_byte - my_low,
        ),
    )
    chooser = (target[:, None] == jnp.arange(3 * rows, dtype=jnp.int32)[None, :]).astype(
        jnp.bfloat16
    )
    spread_back = jnp.dot(chooser, returned, preferred_element_type=jnp.float32)
    byte_lengths = jnp.sum(jnp.where(member, lengths[:, None], 0.0), axis=0)
    byte_grad = (spread_back / byte_lengths[:, None]).astype(jnp.bfloat16)
    return (attn_out, byte_grad)


def solution(mesh):
    placed = (P("ctx", None), P("ctx"), P(), P(), P(None, None, "tp"), P("ctx", "tp"))
    return jax.shard_map(
        shards,
        mesh=mesh,
        in_specs=placed,
        out_specs=(P("ctx", "tp"), P("ctx", "tp")),
        check_vma=False,
    )
```

profile of v0, /device:TPU:6, one launch (start us, length us, event | category | flops | bytes accessed | tf_op | source)
XLA Modules:
  0.0 305.7 jit_solution(10949627991634043434)
XLA Ops:
  8.8 0.9 fusion.56
  9.7 3.4 %collective-permute-start = (bf16[128,512]{1,0:T(8,128)(2,1)S(1)}, bf16[128,512]{1,0:T(8,128)(2,1)S(1)}, u32[]{:S(2)}, u32[]{:S(2)}) collective-permute-start(bf16[128,512]{1,0:T(8,128)(2,1)S(1)} %fusion.56), channel_id=1, source_target_pairs={{0,2},{2,4},{4,6},{6,8},{8,10},{10,12},{12,14},{14,16},{16,18},{18... | collective-permute-start | bytes 393224 | tf_op jit(solution)/shard_map/ppermute | solution.py:16
  13.1 2.4 collective-permute-start.1
  19.2 1.2 dynamic-slice.3
  21.6 1.9 select_bitcast_fusion
  23.8 1.9 all_gather.21
  25.7 2.7 fusion.66
  28.5 2.7 fusion.60
  31.3 2.7 fusion.63
  35.4 36.0 %all-gather.13.cloned.1.call-done = bf16[1024,1024]{1,0:T(8,128)(2,1)} async-done(((bf16[64,1024]{1,0:T(8,128)(2,1)}), bf16[1024,1024]{1,0:T(8,128)(2,1)}) %all-gather.13.cloned.1.call-update) | async-done | bytes 2097168 | tf_op jit(solution)/shard_map/all_gather | solution.py:115
  71.4 2.9 copy.61
  74.3 59.7 %all-gather.9.cloned.1.call-done = bf16[1024,1024]{1,0:T(8,128)(2,1)} async-done(((bf16[64,1024]{1,0:T(8,128)(2,1)}), bf16[1024,1024]{1,0:T(8,128)(2,1)}) %all-gather.9.cloned.1.call-update) | async-done | bytes 2097168 | tf_op jit(solution)/shard_map/all_gather | solution.py:83
  134.0 2.6 select_reduce_fusion
  136.6 1.3 copy-done.2
  138.5 33.8 %all-gather = f32[16,64,8]{1,2,0:T(8,128)S(1)} all-gather(f32[1,64,8]{1,2,0:T(8,128)S(1)} %bitcast.202), channel_id=1, replica_groups=mesh['ctx'=16,'tp'=2] {'ctx'}, dimensions={0}, use_global_device_ids=true | all-gather | bytes 34816 | tf_op jit(solution)/shard_map/all_gather | solution.py:109
  172.4 23.7 %all-gather.7.cloned.1.call-done = bf16[1024,1024]{1,0:T(8,128)(2,1)} async-done(((bf16[64,1024]{1,0:T(8,128)(2,1)}), bf16[1024,1024]{1,0:T(8,128)(2,1)}) %all-gather.7.cloned.1.call-update) | async-done | bytes 2097168 | tf_op jit(solution)/shard_map/all_gather | solution.py:84
  196.2 3.8 %multiply_reduce_fusion = (f32[64,8]{0,1:T(8,128)S(1)}, bf16[8,128,64]{1,2,0:T(8,128)(2,1)}) fusion(f32[8,64,1024]{2,1,0:T(8,128)} %copy-done.2, f32[8,64]{1,0:T(8,128)S(1)} %log_add_fusion, pred[64,1024]{1,0:T(8,128)(4,1)S(1)} %broadcast_compare_fusion.1, bf16[1024,1024]{1,0:T(8,128)(2,1)} %all-gather.7.cloned.1.call-done, bf16[64,1024]{1,0:T(8,128)(2,1)S(1)} %copy-done.6), kind=kOutput, calls=%fused_computation.75 | convolution fusion | flops 136642048 | bytes 4526080 | tf_op jit(solution)/shard_map/hqk,khd->qhd/dot_general | solution.py:96
  200.0 33.9 %all-gather.1 = f32[16,64,8]{1,2,0:T(8,128)S(1)} all-gather(f32[1,64,8]{1,2,0:T(8,128)S(1)} %bitcast.203), channel_id=1, replica_groups=mesh['ctx'=16,'tp'=2] {'ctx'}, dimensions={0}, use_global_device_ids=true | all-gather | bytes 34816 | tf_op jit(solution)/shard_map/all_gather | solution.py:110
  233.9 24.8 %all-gather.11.cloned.1.call-done = bf16[1024,1024]{1,0:T(8,128)(2,1)} async-done(((bf16[64,1024]{1,0:T(8,128)(2,1)}), bf16[1024,1024]{1,0:T(8,128)(2,1)}) %all-gather.11.cloned.1.call-update) | async-done | bytes 2097168 | tf_op jit(solution)/shard_map/all_gather | solution.py:114
  258.7 2.7 select_exponential_fusion
  261.4 0.9 fusion.78
  262.8 3.3 %fusion.75 = bf16[8,8,8,128]{3,2,1,0:T(8,128)(2,1)S(1)} fusion(f32[8,1024,64]{1,2,0:T(8,128)} %copy-done.1, bf16[1024,8,128]{0,2,1:T(8,128)(2,1)S(1)} %bitcast.199, f32[8,1024]{1,0:T(8,128)S(1)} %bitcast.200, bf16[1024,1024]{1,0:T(8,128)(2,1)} %all-gather.11.cloned.1.call-done, bf16[64,1024]{1,0:T(8,128)(2,1)S(1)} %copy-done.4), kind=kOutput, calls=%fused_computation.60 | convolution fusion | flops 270139392 | bytes 6586368 | tf_op jit(solution)/shard_map/hqk,qhd->khd/dot_general | solution.py:133
  266.1 2.5 fusion.14
  268.6 4.0 %fusion.79 = bf16[8,8,8,128]{3,2,1,0:T(8,128)(2,1)S(1)} fusion(f32[8,64,1024]{2,1,0:T(8,128)S(1)} %copy-done.3, f32[8,64]{1,0:T(8,128)S(1)} %bitcast.204, f32[8,64]{1,0:T(8,128)S(1)} %log_add_fusion, pred[64,1024]{1,0:T(8,128)(4,1)S(1)} %broadcast_compare_fusion.1, bf16[1024,1024]{1,0:T(8,128)(2,1)} %all-gather.7.cloned.1.call-done, ...), kind=kOutput, calls=%fused_computation.62 | convolution fusion | flops 271712256 | bytes 6623232 | tf_op jit(solution)/shard_map/hqk,khd->qhd/dot_general | solution.py:105
  272.6 2.4 fusion.47
  275.0 3.1 %fusion.44 = f32[64,1024]{1,0:T(8,128)} fusion(f32[64,1024]{1,0:T(8,128)S(1)} %fusion.47, bf16[3,1024,1024]{2,1,0:T(8,128)(2,1)} %param.10, bf16[8,8,8,128]{3,2,1,0:T(8,128)(2,1)S(1)} %fusion.78), kind=kOutput, calls=%fused_computation.47 | convolution fusion | flops 134283264 | bytes 2752512 | tf_op jit(solution)/shard_map/dot_general | solution.py:144
  283.4 2.6 reduce-scatter.2.cloned.1.call-done
  285.9 0.9 convert_element_type.89
  286.9 3.4 %collective-permute-start.2 = (bf16[64,512]{1,0:T(8,128)(2,1)S(1)}, bf16[64,512]{1,0:T(8,128)(2,1)S(1)}, u32[]{:S(2)}, u32[]{:S(2)}) collective-permute-start(bf16[64,512]{1,0:T(8,128)(2,1)S(1)} %convert_element_type.89), channel_id=1, source_target_pairs={{0,2},{2,4},{4,6},{6,8},{8,10},{10,12},{12,14},{14,16},{16,18},{18... | collective-permute-start | bytes 196616 | tf_op jit(solution)/shard_map/ppermute | solution.py:16
  290.2 2.5 collective-permute-start.3
  293.4 4.8 %collective-permute-done.3 = bf16[64,512]{1,0:T(8,128)(2,1)S(1)} collective-permute-done((bf16[64,512]{1,0:T(8,128)(2,1)S(1)}, bf16[64,512]{1,0:T(8,128)(2,1)S(1)}, u32[]{:S(2)}, u32[]{:S(2)}) %collective-permute-start.3) | collective-permute-done | bytes 65568 | tf_op jit(solution)/shard_map/ppermute | solution.py:17
  298.2 1.0 fusion.43
  (81 shorter events, 12.7 us)
Async XLA Ops:
  7.2 1.6 copy-start
  7.2 64.3 %all-gather.13.cloned.1.call-start = ((), (), s32[]{:S(2)}) async-start(), calls=%async_computation.4 | async-start | bytes 2228224 | tf_op jit(solution)/shard_map/all_gather | solution.py:115
  7.9 126.1 %all-gather.9.cloned.1.call-start = ((), (), s32[]{:S(2)}) async-start(), calls=%async_computation.2 | async-start | bytes 2228224 | tf_op jit(solution)/shard_map/all_gather | solution.py:83
  9.7 13.9 %collective-permute-start = (bf16[128,512]{1,0:T(8,128)(2,1)S(1)}, bf16[128,512]{1,0:T(8,128)(2,1)S(1)}, u32[]{:S(2)}, u32[]{:S(2)}) collective-permute-start(bf16[128,512]{1,0:T(8,128)(2,1)S(1)} %fusion.56), channel_id=1, source_target_pairs={{0,2},{2,4},{4,6},{6,8},{8,10},{10,12},{12,14},{14,16},{16,18},{18... | collective-permute-start | bytes 393224 | tf_op jit(solution)/shard_map/ppermute | solution.py:16
  13.1 10.5 %collective-permute-start.1 = (bf16[128,512]{1,0:T(8,128)(2,1)S(1)}, bf16[128,512]{1,0:T(8,128)(2,1)S(1)}, u32[]{:S(2)}, u32[]{:S(2)}) collective-permute-start(bf16[128,512]{1,0:T(8,128)(2,1)S(1)} %fusion.56), channel_id=1, source_target_pairs={{2,0},{4,2},{6,4},{8,6},{10,8},{12,10},{14,12},{16,14},{18,16},{20... | collective-permute-start | bytes 393224 | tf_op jit(solution)/shard_map/ppermute | solution.py:17
  28.4 167.7 %all-gather.7.cloned.1.call-start = ((), (), s32[]{:S(2)}) async-start(), calls=%async_computation.1 | async-start | bytes 2228224 | tf_op jit(solution)/shard_map/all_gather | solution.py:84
  31.2 3.7 %copy-start.9 = (s32[16]{0:T(128)S(1)}, s32[16]{0:T(128)}, u32[]{:S(2)}) copy-start(s32[16]{0:T(128)} %param.8) | copy-start | bytes 196
  31.2 227.5 %all-gather.11.cloned.1.call-start = ((), (), s32[]{:S(2)}) async-start(), calls=%async_computation.3 | async-start | bytes 2228224 | tf_op jit(solution)/shard_map/all_gather | solution.py:114
  34.0 251.9 %reduce-scatter.2.cloned.1.call-start = ((), (), s32[]{:S(2)}) async-start(), calls=%async_computation.5 | async-start | bytes 393216 | tf_op jit(solution)/shard_map/reduce_scatter | solution.py:147
  35.4 98.6 %copy-start.5 = (bf16[64,1024]{1,0:T(8,128)(2,1)S(1)}, bf16[64,1024]{1,0:T(8,128)(2,1)}, u32[]{:S(2)}) copy-start(bf16[64,1024]{1,0:T(8,128)(2,1)} %fusion.63) | copy-start | bytes 393220
  136.6 1.4 copy-start.2
  136.6 59.6 %copy-start.6 = (bf16[64,1024]{1,0:T(8,128)(2,1)S(1)}, bf16[64,1024]{1,0:T(8,128)(2,1)}, u32[]{:S(2)}) copy-start(bf16[64,1024]{1,0:T(8,128)(2,1)} %param.11) | copy-start | bytes 393220
  172.4 86.3 %copy-start.7 = (bf16[64,1024]{1,0:T(8,128)(2,1)S(1)}, bf16[64,1024]{1,0:T(8,128)(2,1)}, u32[]{:S(2)}) copy-start(bf16[64,1024]{1,0:T(8,128)(2,1)} %fusion.66) | copy-start | bytes 393220
  261.4 1.4 copy-start.1
  261.4 1.4 copy-start.4
  266.1 2.5 copy-start.3
  275.0 7.6 %copy-start.10 = (s32[256]{0:T(256)S(1)}, s32[256]{0:T(256)}, u32[]{:S(2)}) copy-start(s32[256]{0:T(256)} %param.7) | copy-start | bytes 3076
  275.0 17.7 %copy-start.8 = (bf16[8,128,64]{1,2,0:T(8,128)(2,1)S(1)}, bf16[8,128,64]{1,2,0:T(8,128)(2,1)}, u32[]{:S(2)}) copy-start(bf16[8,128,64]{1,2,0:T(8,128)(2,1)} %get-tuple-element.18) | copy-start | bytes 393220
  286.9 6.5 %collective-permute-start.2 = (bf16[64,512]{1,0:T(8,128)(2,1)S(1)}, bf16[64,512]{1,0:T(8,128)(2,1)S(1)}, u32[]{:S(2)}, u32[]{:S(2)}) collective-permute-start(bf16[64,512]{1,0:T(8,128)(2,1)S(1)} %convert_element_type.89), channel_id=1, source_target_pairs={{0,2},{2,4},{4,6},{6,8},{8,10},{10,12},{12,14},{14,16},{16,18},{18... | collective-permute-start | bytes 196616 | tf_op jit(solution)/shard_map/ppermute | solution.py:16
  290.2 8.0 %collective-permute-start.3 = (bf16[64,512]{1,0:T(8,128)(2,1)S(1)}, bf16[64,512]{1,0:T(8,128)(2,1)S(1)}, u32[]{:S(2)}, u32[]{:S(2)}) collective-permute-start(bf16[64,512]{1,0:T(8,128)(2,1)S(1)} %convert_element_type.89), channel_id=1, source_target_pairs={{2,0},{4,2},{6,4},{8,6},{10,8},{12,10},{14,12},{16,14},{18,16},{20... | collective-permute-start | bytes 196616 | tf_op jit(solution)/shard_map/ppermute | solution.py:17
Sparse Core Ops, SparseCore 0:
  10.8 60.6 all-gather.12
  74.8 59.1 all-gather.8
  136.8 59.3 all-gather.6
  199.4 59.2 all-gather.10
  278.3 7.6 reduce-scatter.1
where the time goes:
time: 306 us
  waiting for transfers between devices  152 us (50%)
  blocking collectives  69.5 us (23%)
  matrix products  35.5 us (12%)
  between operations  16.7 us (5%)
  local copies, waits for them, and re-layouts  13.3 us (4%)
  starting transfers between devices  11.9 us (4%)
  other arithmetic  6.49 us (2%)
    all_gather x1, waiting for transfers between devices, shards(): lax.all_gather(keyed, 'ctx', axis=0, tiled=True)  59.7 us
    all_gather x1, waiting for transfers between devices, shards(): g_piece = lax.all_gather(d_attn, 'ctx', axis=0, tiled=True)  36 us
    all_gather x1, blocking collectives, shards(): lax.all_gather(delta, 'ctx', axis=0, tiled=True)  33.9 us
    all_gather x1, blocking collectives, shards(): lax.all_gather(lse_rows, 'ctx', axis=0, tiled=True)  33.8 us
    all_gather x1, waiting for transfers between devices, shards(): q_piece = lax.all_gather(query, 'ctx', axis=0, tiled=True)  24.8 us
    all_gather x1, waiting for transfers between devices, shards(): lax.all_gather(valued, 'ctx', axis=0, tiled=True)  23.7 us
    ppermute x2, starting transfers between devices, extended_2(): before = lax.ppermute(last, axis, up)  6.77 us
  transfers between devices with their start and end apart: 9, of which 6 were waited for; matrix products, arithmetic and copies ran while one was open for 11% of the time, Pallas kernels for 0%

commit v1 on v0

--- a/solution.py
+++ b/solution.py
@@ -4,6 +4,34 @@
 from jax.sharding import PartitionSpec as P
 
 HD = 128
+
+
+def fit_files_for(xx):
+    o_now, piece_next, block_now = (lax.axis_size("ctx"), lax.axis_index("ctx"), xx.shape[0])
+    chunks = []
+    for s, hop_no in enumerate(xx.shape):
+        chunks.append(hop_no * o_now if s == 0 else hop_no)
+    next_value = lax.dynamic_update_slice_in_dim(
+        jnp.zeros(chunks, xx.dtype), xx, piece_next * block_now, axis=0
+    )
+    later = local_out = xx
+    for idx in range(1, o_now // 2 + 1):
+        row_list = []
+        for s in range(o_now):
+            row_list.append((s, (s + 1) % o_now))
+        later = lax.ppermute(later, "ctx", row_list)
+        next_value = lax.dynamic_update_slice_in_dim(
+            next_value, later, (piece_next - idx) % o_now * block_now, axis=0
+        )
+        if 2 * idx < o_now:
+            frames = []
+            for s in range(o_now):
+                frames.append((s, (s - 1) % o_now))
+            local_out = lax.ppermute(local_out, "ctx", frames)
+            next_value = lax.dynamic_update_slice_in_dim(
+                next_value, local_out, (piece_next + idx) % o_now * block_now, axis=0
+            )
+    return next_value
 
 
 def extended_2(x, sides, width):
@@ -79,10 +107,7 @@
     query = jnp.dot(pooled, w_qkv[0], preferred_element_type=jnp.float32).astype(jnp.bfloat16)
     keyed = jnp.dot(pooled, w_qkv[1], preferred_element_type=jnp.float32).astype(jnp.bfloat16)
     valued = jnp.dot(pooled, w_qkv[2], preferred_element_type=jnp.float32).astype(jnp.bfloat16)
-    keys_all, values_all = (
-        lax.all_gather(keyed, "ctx", axis=0, tiled=True),
-        lax.all_gather(valued, "ctx", axis=0, tiled=True),
-    )
+    keys_all, values_all = (lax.all_gather(keyed, "ctx", axis=0, tiled=True), fit_files_for(valued))
     query3 = query.reshape(rows, heads, HD)
     keys3 = keys_all.reshape(total, heads, HD)
     values3 = values_all.reshape(total, heads, HD)

time: 306 us -> 277 us (0.905)
  waiting for transfers between devices: 152 us -> 53 us
  local copies, waits for them, and re-layouts: 13.3 us -> 48.1 us
  starting transfers between devices: 11.9 us -> 44 us
  blocking collectives: 69.5 us -> 75.3 us
  matrix products: 35.5 us -> 32.4 us
    all_gather x1, waiting for transfers between devices: 59.7 us -> 17.1 us  [shards(): lax.all_gather(keyed, 'ctx', axis=0, tiled=True)]
    all_gather x1, waiting for transfers between devices: 36 us -> 0.01 us  [shards(): g_piece = lax.all_gather(d_attn, 'ctx', axis=0, tiled=True)]
    ppermute x0 -> x15, starting transfers between devices: none -> 32.1 us  [the longest x8 29.8 us: fit_files_for(): later = lax.ppermute(later, 'ctx', row_list)]
    ppermute x0 -> x15, waiting for transfers between devices: none -> 26.6 us  [the longest x8 19.4 us: fit_files_for(): later = lax.ppermute(later, 'ctx', row_list)]
    dynamic_update_slice x0 -> x16, local copies, waits for them, and re-layouts: none -> 25.6 us  [the longest x8 12.5 us: fit_files_for(): lax.dynamic_update_slice_in_dim(next_value, later, (piece_next - idx) % o...]
    all_gather x1, waiting for transfers between devices: 24.8 us -> 0.01 us  [shards(): q_piece = lax.all_gather(query, 'ctx', axis=0, tiled=True)]
    all_gather x1 -> x0, waiting for transfers between devices: 23.7 us -> none  [shards(): lax.all_gather(valued, 'ctx', axis=0, tiled=True)]
    ppermute x0 -> x15, local copies, waits for them, and re-layouts: none -> 6.14 us  [the longest x8 3.15 us: fit_files_for(): later = lax.ppermute(later, 'ctx', row_list)]
  transfers between devices with their start and end apart: 9 -> 23, of which waited for: 6 -> 13; matrix products, arithmetic and copies ran while one was open for 11% -> 23% of each run, Pallas kernels for 0% -> 0%
where the time goes in v1:
time: 277 us; the launch traced here: 276 us
  blocking collectives  75.3 us (27%)
  waiting for transfers between devices  53 us (19%)
  local copies, waits for them, and re-layouts  48.1 us (17%)
  starting transfers between devices  44 us (16%)
  matrix products  32.4 us (12%)
  between operations  17.1 us (6%)
  other arithmetic  6.39 us (2%)
    all_gather x1, blocking collectives, shards(): lax.all_gather(lse_rows, 'ctx', axis=0, tiled=True)  39.5 us
    all_gather x1, blocking collectives, shards(): lax.all_gather(delta, 'ctx', axis=0, tiled=True)  33.9 us
    ppermute x8, starting transfers between devices, fit_files_for(): later = lax.ppermute(later, 'ctx', row_list)  29.8 us
    ppermute x8, waiting for transfers between devices, fit_files_for(): later = lax.ppermute(later, 'ctx', row_list)  19.4 us
    all_gather x1, waiting for transfers between devices, shards(): lax.all_gather(keyed, 'ctx', axis=0, tiled=True)  17.1 us
    dynamic_update_slice x8, local copies, waits for them, and re-layouts, fit_files_for(): lax.dynamic_update_slice_in_dim(next_value, later, (piece_next - idx) % o...  12.5 us
    dynamic_update_slice x7, local copies, waits for them, and re-layouts, fit_files_for(): lax.dynamic_update_slice_in_dim(next_value, local_out, (piece_next + idx)...  11.1 us
    ppermute x7, waiting for transfers between devices, fit_files_for(): local_out = lax.ppermute(local_out, 'ctx', frames)  7.2 us
  transfers between devices with their start and end apart: 23, of which 13 were waited for; matrix products, arithmetic and copies ran while one was open for 23% of the time, Pallas kernels for 0%

profile of v1, /device:TPU:6, one launch (start us, length us, event | category | flops | bytes accessed | tf_op | source)
XLA Modules:
  0.0 276.3 jit_solution(8172281466722485719)
XLA Ops:
  9.7 3.4 %collective-permute-start = (bf16[128,512]{1,0:T(8,128)(2,1)S(1)}, bf16[128,512]{1,0:T(8,128)(2,1)S(1)}, u32[]{:S(2)}, u32[]{:S(2)}) collective-permute-start(bf16[128,512]{1,0:T(8,128)(2,1)S(1)} %fusion.48), channel_id=1, source_target_pairs={{0,2},{2,4},{4,6},{6,8},{8,10},{10,12},{12,14},{14,16},{16,18},{18... | collective-permute-start | bytes 393224 | tf_op jit(solution)/shard_map/ppermute | solution.py:44
  13.1 2.4 collective-permute-start.1
  26.4 2.7 fusion.58
  29.2 2.7 fusion.55
  34.1 3.3 %collective-permute-start.2 = (bf16[64,1024]{1,0:T(8,128)(2,1)S(1)}, bf16[64,1024]{1,0:T(8,128)(2,1)S(1)}, u32[]{:S(2)}, u32[]{:S(2)}) collective-permute-start(bf16[64,1024]{1,0:T(8,128)(2,1)S(1)} %fusion.52), channel_id=1, source_target_pairs={{0,2},{2,4},{4,6},{6,8},{8,10},{10,12},{12,14},{14,16},{16,18},{18... | collective-permute-start | bytes 393224 | tf_op jit(solution)/shard_map/ppermute | solution.py:22
  37.4 5.2 %collective-permute-done.2 = bf16[64,1024]{1,0:T(8,128)(2,1)S(1)} collective-permute-done((bf16[64,1024]{1,0:T(8,128)(2,1)S(1)}, bf16[64,1024]{1,0:T(8,128)(2,1)S(1)}, u32[]{:S(2)}, u32[]{:S(2)}) %collective-permute-start.2) | collective-permute-done | bytes 131104 | tf_op jit(solution)/shard_map/ppermute | solution.py:22
  42.6 3.6 %collective-permute-start.4 = (bf16[64,1024]{1,0:T(8,128)(2,1)S(1)}, bf16[64,1024]{1,0:T(8,128)(2,1)S(1)}, u32[]{:S(2)}, u32[]{:S(2)}) collective-permute-start(bf16[64,1024]{1,0:T(8,128)(2,1)S(1)} %collective-permute-done.2), channel_id=1, source_target_pairs={{0,2},{2,4},{4,6},{6,8},{8,10},{10,12},{12,14},{14,16},{16,18},{18... | collective-permute-start | bytes 393224 | tf_op jit(solution)/shard_map/ppermute | solution.py:22
  50.9 4.3 %collective-permute-start.6 = (bf16[64,1024]{1,0:T(8,128)(2,1)S(1)}, bf16[64,1024]{1,0:T(8,128)(2,1)S(1)}, u32[]{:S(2)}, u32[]{:S(2)}) collective-permute-start(bf16[64,1024]{1,0:T(8,128)(2,1)S(1)} %collective-permute-done.4), channel_id=1, source_target_pairs={{0,2},{2,4},{4,6},{6,8},{8,10},{10,12},{12,14},{14,16},{16,18},{18... | collective-permute-start | bytes 393224 | tf_op jit(solution)/shard_map/ppermute | solution.py:22
  55.2 2.5 collective-permute-done.6
  57.7 4.2 %collective-permute-start.8 = (bf16[64,1024]{1,0:T(8,128)(2,1)S(1)}, bf16[64,1024]{1,0:T(8,128)(2,1)S(1)}, u32[]{:S(2)}, u32[]{:S(2)}) collective-permute-start(bf16[64,1024]{1,0:T(8,128)(2,1)S(1)} %collective-permute-done.6), channel_id=1, source_target_pairs={{0,2},{2,4},{4,6},{6,8},{8,10},{10,12},{12,14},{14,16},{16,18},{18... | collective-permute-start | bytes 393224 | tf_op jit(solution)/shard_map/ppermute | solution.py:22
  62.5 5.1 %collective-permute-done.8 = bf16[64,1024]{1,0:T(8,128)(2,1)S(1)} collective-permute-done((bf16[64,1024]{1,0:T(8,128)(2,1)S(1)}, bf16[64,1024]{1,0:T(8,128)(2,1)S(1)}, u32[]{:S(2)}, u32[]{:S(2)}) %collective-permute-start.8) | collective-permute-done | bytes 131104 | tf_op jit(solution)/shard_map/ppermute | solution.py:22
  67.7 4.3 %collective-permute-start.10 = (bf16[64,1024]{1,0:T(8,128)(2,1)S(1)}, bf16[64,1024]{1,0:T(8,128)(2,1)S(1)}, u32[]{:S(2)}, u32[]{:S(2)}) collective-permute-start(bf16[64,1024]{1,0:T(8,128)(2,1)S(1)} %collective-permute-done.8), channel_id=1, source_target_pairs={{0,2},{2,4},{4,6},{6,8},{8,10},{10,12},{12,14},{14,16},{16,18},{18... | collective-permute-start | bytes 393224 | tf_op jit(solution)/shard_map/ppermute | solution.py:22
  73.1 3.3 %collective-permute-done.10 = bf16[64,1024]{1,0:T(8,128)(2,1)S(1)} collective-permute-done((bf16[64,1024]{1,0:T(8,128)(2,1)S(1)}, bf16[64,1024]{1,0:T(8,128)(2,1)S(1)}, u32[]{:S(2)}, u32[]{:S(2)}) %collective-permute-start.10) | collective-permute-done | bytes 131104 | tf_op jit(solution)/shard_map/ppermute | solution.py:22
  76.4 3.2 %collective-permute-start.12 = (bf16[64,1024]{1,0:T(8,128)(2,1)S(1)}, bf16[64,1024]{1,0:T(8,128)(2,1)S(1)}, u32[]{:S(2)}, u32[]{:S(2)}) collective-permute-start(bf16[64,1024]{1,0:T(8,128)(2,1)S(1)} %collective-permute-done.10), channel_id=1, source_target_pairs={{0,2},{2,4},{4,6},{6,8},{8,10},{10,12},{12,14},{14,16},{16,18},{18... | collective-permute-start | bytes 393224 | tf_op jit(solution)/shard_map/ppermute | solution.py:22
  79.7 2.9 %collective-permute-done.11 = bf16[64,1024]{1,0:T(8,128)(2,1)S(1)} collective-permute-done((bf16[64,1024]{1,0:T(8,128)(2,1)S(1)}, bf16[64,1024]{1,0:T(8,128)(2,1)S(1)}, u32[]{:S(2)}, u32[]{:S(2)}) %collective-permute-start.11) | collective-permute-done | bytes 131104 | tf_op jit(solution)/shard_map/ppermute | solution.py:30
  82.7 3.7 %collective-permute-start.14 = (bf16[64,1024]{1,0:T(8,128)(2,1)S(1)}, bf16[64,1024]{1,0:T(8,128)(2,1)}, u32[]{:S(2)}, u32[]{:S(2)}) collective-permute-start(bf16[64,1024]{1,0:T(8,128)(2,1)S(1)} %collective-permute-done.12), channel_id=1, source_target_pairs={{0,2},{2,4},{4,6},{6,8},{8,10},{10,12},{12,14},{14,16},{16,18},{18... | collective-permute-start | bytes 393224 | tf_op jit(solution)/shard_map/ppermute | solution.py:22
  86.5 3.7 %collective-permute-done.13 = bf16[64,1024]{1,0:T(8,128)(2,1)} collective-permute-done((bf16[64,1024]{1,0:T(8,128)(2,1)S(1)}, bf16[64,1024]{1,0:T(8,128)(2,1)}, u32[]{:S(2)}, u32[]{:S(2)}) %collective-permute-start.13) | collective-permute-done | bytes 131104 | tf_op jit(solution)/shard_map/ppermute | solution.py:30
  91.0 3.1 %collective-permute-start.16 = (bf16[64,1024]{1,0:T(8,128)(2,1)}, bf16[64,1024]{1,0:T(8,128)(2,1)}, u32[]{:S(2)}, u32[]{:S(2)}) collective-permute-start(bf16[64,1024]{1,0:T(8,128)(2,1)} %collective-permute-done.14), channel_id=1, source_target_pairs={{0,2},{2,4},{4,6},{6,8},{8,10},{10,12},{12,14},{14,16},{16,18},{18... | collective-permute-start | bytes 393224 | tf_op jit(solution)/shard_map/ppermute | solution.py:22
  128.3 2.9 %copy.108 = bf16[1024,1024]{0,1:T(8,128)(2,1)S(1)} copy(bf16[1024,1024]{1,0:T(8,128)(2,1)} %all-gather.10.cloned.1.call-done) | data formatting | bytes 4194304 | tf_op jit(solution)/shard_map/all_gather | solution.py:140
  131.2 17.1 %all-gather.6.cloned.1.call-done = bf16[1024,1024]{1,0:T(8,128)(2,1)} async-done(((bf16[64,1024]{1,0:T(8,128)(2,1)}), bf16[1024,1024]{1,0:T(8,128)(2,1)}) %all-gather.6.cloned.1.call-update) | async-done | bytes 2097168 | tf_op jit(solution)/shard_map/all_gather | solution.py:110
  148.3 2.6 select_reduce_fusion
  154.9 33.9 %all-gather.1 = f32[16,64,8]{1,2,0:T(8,128)S(1)} all-gather(f32[1,64,8]{1,2,0:T(8,128)S(1)} %bitcast.187), channel_id=1, replica_groups=mesh['ctx'=16,'tp'=2] {'ctx'}, dimensions={0}, use_global_device_ids=true | all-gather | bytes 34816 | tf_op jit(solution)/shard_map/all_gather | solution.py:135
  188.9 39.5 %all-gather = f32[16,64,8]{1,2,0:T(8,128)S(1)} all-gather(f32[1,64,8]{1,2,0:T(8,128)S(1)} %bitcast.186), channel_id=1, replica_groups=mesh['ctx'=16,'tp'=2] {'ctx'}, dimensions={0}, use_global_device_ids=true | all-gather | bytes 34816 | tf_op jit(solution)/shard_map/all_gather | solution.py:134
  228.5 2.7 select_exponential_fusion
  232.5 3.3 %fusion.64 = bf16[8,8,8,128]{3,2,1,0:T(8,128)(2,1)S(1)} fusion(f32[8,1024,64]{1,2,0:T(8,128)} %copy-done.1, bf16[1024,8,128]{0,2,1:T(8,128)(2,1)S(1)} %bitcast.181, f32[8,1024]{1,0:T(8,128)S(1)} %bitcast.184, bf16[1024,1024]{1,0:T(8,128)(2,1)} %all-gather.8.cloned.1.call-done, bf16[64,1024]{1,0:T(8,128)(2,1)S(1)} %fusion.52), kind=kOutput, calls=%fused_computation.54 | convolution fusion | flops 270139392 | bytes 6586368 | tf_op jit(solution)/shard_map/hqk,qhd->khd/dot_general | solution.py:158
  235.9 2.5 fusion.10
  238.4 3.7 %fusion.68 = bf16[8,8,8,128]{3,2,1,0:T(8,128)(2,1)S(1)} fusion(bf16[1024,8,128]{0,2,1:T(8,128)(2,1)} %bitcast.182, f32[8,64,1024]{2,1,0:T(8,128)S(1)} %copy-done.3, f32[8,64]{1,0:T(8,128)S(1)} %bitcast.188, f32[8,64]{1,0:T(8,128)S(1)} %log_add_fusion, pred[64,1024]{1,0:T(8,128)(4,1)S(1)} %broadcast_compare_fusion.1, ...), kind=kOutput, calls=%fused_computation.56 | convolution fusion | flops 271712256 | bytes 6623232 | tf_op jit(solution)/shard_map/hqk,khd->qhd/dot_general | solution.py:130
  244.5 3.1 %fusion.36 = f32[64,1024]{1,0:T(8,128)} fusion(f32[64,1024]{1,0:T(8,128)S(1)} %fusion.39, bf16[3,1024,1024]{2,1,0:T(8,128)(2,1)} %param.10, bf16[8,8,8,128]{3,2,1,0:T(8,128)(2,1)S(1)} %fusion.67), kind=kOutput, calls=%fused_computation.41 | convolution fusion | flops 134283264 | bytes 2752512 | tf_op jit(solution)/shard_map/dot_general | solution.py:169
  252.8 3.7 %reduce-scatter.2.cloned.1.call-done = f32[64,512]{1,0:T(8,128)} async-done(((f32[64,1024]{1,0:T(8,128)}), f32[64,512]{1,0:T(8,128)}) %reduce-scatter.2.cloned.1.call-update) | async-done | bytes 131088 | tf_op jit(solution)/shard_map/reduce_scatter | solution.py:172
  257.4 3.4 %collective-permute-start.17 = (bf16[64,512]{1,0:T(8,128)(2,1)S(1)}, bf16[64,512]{1,0:T(8,128)(2,1)S(1)}, u32[]{:S(2)}, u32[]{:S(2)}) collective-permute-start(bf16[64,512]{1,0:T(8,128)(2,1)S(1)} %convert_element_type.89), channel_id=1, source_target_pairs={{0,2},{2,4},{4,6},{6,8},{8,10},{10,12},{12,14},{14,16},{16,18},{18... | collective-permute-start | bytes 196616 | tf_op jit(solution)/shard_map/ppermute | solution.py:44
  260.8 2.5 collective-permute-start.18
  264.0 4.8 %collective-permute-done.18 = bf16[64,512]{1,0:T(8,128)(2,1)S(1)} collective-permute-done((bf16[64,512]{1,0:T(8,128)(2,1)S(1)}, bf16[64,512]{1,0:T(8,128)(2,1)S(1)}, u32[]{:S(2)}, u32[]{:S(2)}) %collective-permute-start.18) | collective-permute-done | bytes 65568 | tf_op jit(solution)/shard_map/ppermute | solution.py:45
  (183 shorter events, 69.6 us)
Async XLA Ops:
  7.2 121.1 %all-gather.10.cloned.1.call-start = ((), (), s32[]{:S(2)}) async-start(), calls=%async_computation.3 | async-start | bytes 2228224 | tf_op jit(solution)/shard_map/all_gather | solution.py:140
  7.9 140.4 %all-gather.6.cloned.1.call-start = ((), (), s32[]{:S(2)}) async-start(), calls=%async_computation.1 | async-start | bytes 2228224 | tf_op jit(solution)/shard_map/all_gather | solution.py:110
  9.7 14.6 %collective-permute-start = (bf16[128,512]{1,0:T(8,128)(2,1)S(1)}, bf16[128,512]{1,0:T(8,128)(2,1)S(1)}, u32[]{:S(2)}, u32[]{:S(2)}) collective-permute-start(bf16[128,512]{1,0:T(8,128)(2,1)S(1)} %fusion.48), channel_id=1, source_target_pairs={{0,2},{2,4},{4,6},{6,8},{8,10},{10,12},{12,14},{14,16},{16,18},{18... | collective-permute-start | bytes 393224 | tf_op jit(solution)/shard_map/ppermute | solution.py:44
  13.1 11.2 %collective-permute-start.1 = (bf16[128,512]{1,0:T(8,128)(2,1)S(1)}, bf16[128,512]{1,0:T(8,128)(2,1)S(1)}, u32[]{:S(2)}, u32[]{:S(2)}) collective-permute-start(bf16[128,512]{1,0:T(8,128)(2,1)S(1)} %fusion.48), channel_id=1, source_target_pairs={{2,0},{4,2},{6,4},{8,6},{10,8},{12,10},{14,12},{16,14},{18,16},{20... | collective-permute-start | bytes 393224 | tf_op jit(solution)/shard_map/ppermute | solution.py:45
  29.1 199.4 %all-gather.8.cloned.1.call-start = ((), (), s32[]{:S(2)}) async-start(), calls=%async_computation.2 | async-start | bytes 2228224 | tf_op jit(solution)/shard_map/all_gather | solution.py:139
  31.9 40.9 %copy-start.26 = (s32[16]{0:T(128)S(1)}, s32[16]{0:T(128)}, u32[]{:S(2)}) copy-start(s32[16]{0:T(128)} %param.8) | copy-start | bytes 196
  31.9 224.6 %reduce-scatter.2.cloned.1.call-start = ((), (), s32[]{:S(2)}) async-start(), calls=%async_computation.4 | async-start | bytes 393216 | tf_op jit(solution)/shard_map/reduce_scatter | solution.py:172
  34.1 8.5 %collective-permute-start.2 = (bf16[64,1024]{1,0:T(8,128)(2,1)S(1)}, bf16[64,1024]{1,0:T(8,128)(2,1)S(1)}, u32[]{:S(2)}, u32[]{:S(2)}) collective-permute-start(bf16[64,1024]{1,0:T(8,128)(2,1)S(1)} %fusion.52), channel_id=1, source_target_pairs={{0,2},{2,4},{4,6},{6,8},{8,10},{10,12},{12,14},{14,16},{16,18},{18... | collective-permute-start | bytes 393224 | tf_op jit(solution)/shard_map/ppermute | solution.py:22
  37.4 8.9 %collective-permute-start.3 = (bf16[64,1024]{1,0:T(8,128)(2,1)S(1)}, bf16[64,1024]{1,0:T(8,128)(2,1)S(1)}, u32[]{:S(2)}, u32[]{:S(2)}) collective-permute-start(bf16[64,1024]{1,0:T(8,128)(2,1)S(1)} %fusion.52), channel_id=1, source_target_pairs={{0,30},{2,0},{4,2},{6,4},{8,6},{10,8},{12,10},{14,12},{16,14},{18,... | collective-permute-start | bytes 393224 | tf_op jit(solution)/shard_map/ppermute | solution.py:30
  42.6 8.3 %collective-permute-start.4 = (bf16[64,1024]{1,0:T(8,128)(2,1)S(1)}, bf16[64,1024]{1,0:T(8,128)(2,1)S(1)}, u32[]{:S(2)}, u32[]{:S(2)}) collective-permute-start(bf16[64,1024]{1,0:T(8,128)(2,1)S(1)} %collective-permute-done.2), channel_id=1, source_target_pairs={{0,2},{2,4},{4,6},{6,8},{8,10},{10,12},{12,14},{14,16},{16,18},{18... | collective-permute-start | bytes 393224 | tf_op jit(solution)/shard_map/ppermute | solution.py:22
  46.3 8.9 %collective-permute-start.5 = (bf16[64,1024]{1,0:T(8,128)(2,1)S(1)}, bf16[64,1024]{1,0:T(8,128)(2,1)S(1)}, u32[]{:S(2)}, u32[]{:S(2)}) collective-permute-start(bf16[64,1024]{1,0:T(8,128)(2,1)S(1)} %collective-permute-done.3), channel_id=1, source_target_pairs={{0,30},{2,0},{4,2},{6,4},{8,6},{10,8},{12,10},{14,12},{16,14},{18,... | collective-permute-start | bytes 393224 | tf_op jit(solution)/shard_map/ppermute | solution.py:30
  50.9 6.8 %collective-permute-start.6 = (bf16[64,1024]{1,0:T(8,128)(2,1)S(1)}, bf16[64,1024]{1,0:T(8,128)(2,1)S(1)}, u32[]{:S(2)}, u32[]{:S(2)}) collective-permute-start(bf16[64,1024]{1,0:T(8,128)(2,1)S(1)} %collective-permute-done.4), channel_id=1, source_target_pairs={{0,2},{2,4},{4,6},{6,8},{8,10},{10,12},{12,14},{14,16},{16,18},{18... | collective-permute-start | bytes 393224 | tf_op jit(solution)/shard_map/ppermute | solution.py:22
  55.2 7.3 %collective-permute-start.7 = (bf16[64,1024]{1,0:T(8,128)(2,1)S(1)}, bf16[64,1024]{1,0:T(8,128)(2,1)S(1)}, u32[]{:S(2)}, u32[]{:S(2)}) collective-permute-start(bf16[64,1024]{1,0:T(8,128)(2,1)S(1)} %collective-permute-done.5), channel_id=1, source_target_pairs={{0,30},{2,0},{4,2},{6,4},{8,6},{10,8},{12,10},{14,12},{16,14},{18,... | collective-permute-start | bytes 393224 | tf_op jit(solution)/shard_map/ppermute | solution.py:30
  57.7 10.0 %collective-permute-start.8 = (bf16[64,1024]{1,0:T(8,128)(2,1)S(1)}, bf16[64,1024]{1,0:T(8,128)(2,1)S(1)}, u32[]{:S(2)}, u32[]{:S(2)}) collective-permute-start(bf16[64,1024]{1,0:T(8,128)(2,1)S(1)} %collective-permute-done.6), channel_id=1, source_target_pairs={{0,2},{2,4},{4,6},{6,8},{8,10},{10,12},{12,14},{14,16},{16,18},{18... | collective-permute-start | bytes 393224 | tf_op jit(solution)/shard_map/ppermute | solution.py:22
  62.5 31.7 %copy-start.11 = (bf16[64,1024]{1,0:T(8,128)(2,1)}, bf16[64,1024]{1,0:T(8,128)(2,1)S(1)}, u32[]{:S(2)}) copy-start(bf16[64,1024]{1,0:T(8,128)(2,1)S(1)} %collective-permute-done.7) | copy-start | bytes 393220
  62.5 10.5 %collective-permute-start.9 = (bf16[64,1024]{1,0:T(8,128)(2,1)S(1)}, bf16[64,1024]{1,0:T(8,128)(2,1)S(1)}, u32[]{:S(2)}, u32[]{:S(2)}) collective-permute-start(bf16[64,1024]{1,0:T(8,128)(2,1)S(1)} %collective-permute-done.7), channel_id=1, source_target_pairs={{0,30},{2,0},{4,2},{6,4},{8,6},{10,8},{12,10},{14,12},{16,14},{18,... | collective-permute-start | bytes 393224 | tf_op jit(solution)/shard_map/ppermute | solution.py:30
  67.7 26.5 %copy-start.13 = (bf16[64,1024]{1,0:T(8,128)(2,1)}, bf16[64,1024]{1,0:T(8,128)(2,1)S(1)}, u32[]{:S(2)}) copy-start(bf16[64,1024]{1,0:T(8,128)(2,1)S(1)} %collective-permute-done.8) | copy-start | bytes 393220
  67.7 8.7 %collective-permute-start.10 = (bf16[64,1024]{1,0:T(8,128)(2,1)S(1)}, bf16[64,1024]{1,0:T(8,128)(2,1)S(1)}, u32[]{:S(2)}, u32[]{:S(2)}) collective-permute-start(bf16[64,1024]{1,0:T(8,128)(2,1)S(1)} %collective-permute-done.8), channel_id=1, source_target_pairs={{0,2},{2,4},{4,6},{6,8},{8,10},{10,12},{12,14},{14,16},{16,18},{18... | collective-permute-start | bytes 393224 | tf_op jit(solution)/shard_map/ppermute | solution.py:22
  73.1 21.2 %copy-start.15 = (bf16[64,1024]{1,0:T(8,128)(2,1)}, bf16[64,1024]{1,0:T(8,128)(2,1)S(1)}, u32[]{:S(2)}) copy-start(bf16[64,1024]{1,0:T(8,128)(2,1)S(1)} %collective-permute-done.9) | copy-start | bytes 393220
  73.1 9.5 %collective-permute-start.11 = (bf16[64,1024]{1,0:T(8,128)(2,1)S(1)}, bf16[64,1024]{1,0:T(8,128)(2,1)S(1)}, u32[]{:S(2)}, u32[]{:S(2)}) collective-permute-start(bf16[64,1024]{1,0:T(8,128)(2,1)S(1)} %collective-permute-done.9), channel_id=1, source_target_pairs={{0,30},{2,0},{4,2},{6,4},{8,6},{10,8},{12,10},{14,12},{16,14},{18,... | collective-permute-start | bytes 393224 | tf_op jit(solution)/shard_map/ppermute | solution.py:30
  76.4 17.8 %copy-start.17 = (bf16[64,1024]{1,0:T(8,128)(2,1)}, bf16[64,1024]{1,0:T(8,128)(2,1)S(1)}, u32[]{:S(2)}) copy-start(bf16[64,1024]{1,0:T(8,128)(2,1)S(1)} %collective-permute-done.10) | copy-start | bytes 393220
  76.4 6.3 %collective-permute-start.12 = (bf16[64,1024]{1,0:T(8,128)(2,1)S(1)}, bf16[64,1024]{1,0:T(8,128)(2,1)S(1)}, u32[]{:S(2)}, u32[]{:S(2)}) collective-permute-start(bf16[64,1024]{1,0:T(8,128)(2,1)S(1)} %collective-permute-done.10), channel_id=1, source_target_pairs={{0,2},{2,4},{4,6},{6,8},{8,10},{10,12},{12,14},{14,16},{16,18},{18... | collective-permute-start | bytes 393224 | tf_op jit(solution)/shard_map/ppermute | solution.py:22
  82.5 11.7 %copy-start.19 = (bf16[64,1024]{1,0:T(8,128)(2,1)}, bf16[64,1024]{1,0:T(8,128)(2,1)S(1)}, u32[]{:S(2)}) copy-start(bf16[64,1024]{1,0:T(8,128)(2,1)S(1)} %collective-permute-done.11) | copy-start | bytes 393220
  82.5 7.7 %collective-permute-start.13 = (bf16[64,1024]{1,0:T(8,128)(2,1)S(1)}, bf16[64,1024]{1,0:T(8,128)(2,1)}, u32[]{:S(2)}, u32[]{:S(2)}) collective-permute-start(bf16[64,1024]{1,0:T(8,128)(2,1)S(1)} %collective-permute-done.11), channel_id=1, source_target_pairs={{0,30},{2,0},{4,2},{6,4},{8,6},{10,8},{12,10},{14,12},{16,14},{18,... | collective-permute-start | bytes 393224 | tf_op jit(solution)/shard_map/ppermute | solution.py:30
  82.7 8.3 %collective-permute-start.14 = (bf16[64,1024]{1,0:T(8,128)(2,1)S(1)}, bf16[64,1024]{1,0:T(8,128)(2,1)}, u32[]{:S(2)}, u32[]{:S(2)}) collective-permute-start(bf16[64,1024]{1,0:T(8,128)(2,1)S(1)} %collective-permute-done.12), channel_id=1, source_target_pairs={{0,2},{2,4},{4,6},{6,8},{8,10},{10,12},{12,14},{14,16},{16,18},{18... | collective-permute-start | bytes 393224 | tf_op jit(solution)/shard_map/ppermute | solution.py:22
  90.3 31.2 %collective-permute-start.15 = (bf16[64,1024]{1,0:T(8,128)(2,1)}, bf16[64,1024]{1,0:T(8,128)(2,1)}, u32[]{:S(2)}, u32[]{:S(2)}) collective-permute-start(bf16[64,1024]{1,0:T(8,128)(2,1)} %collective-permute-done.13), channel_id=1, source_target_pairs={{0,30},{2,0},{4,2},{6,4},{8,6},{10,8},{12,10},{14,12},{16,14},{18,... | collective-permute-start | bytes 393224 | tf_op jit(solution)/shard_map/ppermute | solution.py:30
  91.0 32.7 %collective-permute-start.16 = (bf16[64,1024]{1,0:T(8,128)(2,1)}, bf16[64,1024]{1,0:T(8,128)(2,1)}, u32[]{:S(2)}, u32[]{:S(2)}) collective-permute-start(bf16[64,1024]{1,0:T(8,128)(2,1)} %collective-permute-done.14), channel_id=1, source_target_pairs={{0,2},{2,4},{4,6},{6,8},{8,10},{10,12},{12,14},{14,16},{16,18},{18... | collective-permute-start | bytes 393224 | tf_op jit(solution)/shard_map/ppermute | solution.py:22
  128.3 20.0 %copy-start.6 = (bf16[64,1024]{1,0:T(8,128)(2,1)S(1)}, bf16[64,1024]{1,0:T(8,128)(2,1)}, u32[]{:S(2)}) copy-start(bf16[64,1024]{1,0:T(8,128)(2,1)} %fusion.55) | copy-start | bytes 393220
  153.3 75.2 %copy-start.24 = (bf16[64,1024]{1,0:T(8,128)(2,1)S(1)}, bf16[64,1024]{1,0:T(8,128)(2,1)}, u32[]{:S(2)}) copy-start(bf16[64,1024]{1,0:T(8,128)(2,1)} %fusion.58) | copy-start | bytes 393220
  244.5 18.8 %copy-start.25 = (bf16[8,128,64]{1,2,0:T(8,128)(2,1)S(1)}, bf16[8,128,64]{1,2,0:T(8,128)(2,1)}, u32[]{:S(2)}) copy-start(bf16[8,128,64]{1,2,0:T(8,128)(2,1)} %get-tuple-element.18) | copy-start | bytes 393220
  257.4 6.5 %collective-permute-start.17 = (bf16[64,512]{1,0:T(8,128)(2,1)S(1)}, bf16[64,512]{1,0:T(8,128)(2,1)S(1)}, u32[]{:S(2)}, u32[]{:S(2)}) collective-permute-start(bf16[64,512]{1,0:T(8,128)(2,1)S(1)} %convert_element_type.89), channel_id=1, source_target_pairs={{0,2},{2,4},{4,6},{6,8},{8,10},{10,12},{12,14},{14,16},{16,18},{18... | collective-permute-start | bytes 196616 | tf_op jit(solution)/shard_map/ppermute | solution.py:44
  260.8 8.0 %collective-permute-start.18 = (bf16[64,512]{1,0:T(8,128)(2,1)S(1)}, bf16[64,512]{1,0:T(8,128)(2,1)S(1)}, u32[]{:S(2)}, u32[]{:S(2)}) collective-permute-start(bf16[64,512]{1,0:T(8,128)(2,1)S(1)} %convert_element_type.89), channel_id=1, source_target_pairs={{2,0},{4,2},{6,4},{8,6},{10,8},{12,10},{14,12},{16,14},{18,16},{20... | collective-permute-start | bytes 196616 | tf_op jit(solution)/shard_map/ppermute | solution.py:45
  (23 other events, 111.6 us)
Sparse Core Ops, SparseCore 0:
  10.8 74.0 all-gather.9
  87.6 60.6 all-gather.5
  151.1 59.5 all-gather.7
  247.7 8.7 reduce-scatter.1
